TPU v7x, 32 devices: a whole 2x2x4 slice. The times are simulated.
32 devices in a mesh: gx: 16 (over z, y, x), gy: 1, gz: 2 (over core).
Axes of the slice: x: 2, y: 2, z: 4, core: 2. Of those that a mesh axis runs over, the one named last changes fastest.
Arguments:
- populations: float32 [19, 128, 8, 256], P(None, 'gx', 'gy', 'gz'), may hold values from 0.01 to 0.11
Outputs:
- populations_next: float32 [19, 128, 8, 256], P(None, 'gx', 'gy', 'gz')
- moments_slab: float32 [4, 256, 8, 128], P(None, ('gz', 'gx'), 'gy')
All inputs are finite; a program needn't handle non-finite values.
Results may differ from a plain program's by a relative error of at most 0.0003.
Values sent between devices are 32-bit elements; how exact they have to be, the bound alone decides.
A program may use at most 64 MiB of HBM per device.

v0:
```python
from functools import reduce
import jax
import jax.numpy as jnp
from jax import lax
from jax.sharding import PartitionSpec as P

lattice_moves = [
    (0, 0, 0),
    (1, 0, 0),
    (-1, 0, 0),
    (0, 1, 0),
    (0, -1, 0),
    (0, 0, 1),
    (0, 0, -1),
    (1, 1, 0),
    (-1, -1, 0),
    (1, -1, 0),
    (-1, 1, 0),
    (1, 0, 1),
    (-1, 0, -1),
    (1, 0, -1),
    (-1, 0, 1),
    (0, 1, 1),
    (0, -1, -1),
    (0, 1, -1),
    (0, -1, 1),
]
lattice_weights = [1.0 / 3.0] + [1.0 / 18.0] * 6 + [1.0 / 36.0] * 12
relaxation = 1.6


def with_halo(x, sides, width):
    for axis, dim in sides:
        count, length = (lax.axis_size(axis), x.shape[dim])
        up = [(i, (i + 1) % count) for i in range(count)]
        down = [(j, i) for i, j in up]
        last = lax.slice_in_dim(x, length - width, length, axis=dim)
        leading = lax.slice_in_dim(x, 0, width, axis=dim)
        before = lax.ppermute(last, axis, up)
        after = lax.ppermute(leading, axis, down)
        x = jnp.concatenate([before, x, after], axis=dim)
    return x


def signed_total(pieces, component):
    total = jnp.zeros_like(pieces[0])
    for move, piece in zip(lattice_moves, pieces):
        if move[component] == 1:
            total = total + piece
        elif move[component] == -1:
            total = total - piece
    return total


def lattice_moments(pieces):
    density = reduce(lambda left, right: left + right, pieces)
    velocity_x = signed_total(pieces, 0) / density
    velocity_y = signed_total(pieces, 1) / density
    velocity_z = signed_total(pieces, 2) / density
    return (density, velocity_x, velocity_y, velocity_z)


def collide(pieces):
    density, velocity_x, velocity_y, velocity_z = lattice_moments(pieces)
    speed_sq = velocity_x * velocity_x + velocity_y * velocity_y + velocity_z * velocity_z
    result = []
    for move, weight, piece in zip(lattice_moves, lattice_weights, pieces):
        projected = move[0] * velocity_x + move[1] * velocity_y + move[2] * velocity_z
        balance = (
            weight
            * density
            * (1.0 + 3.0 * projected + 4.5 * projected * projected - 1.5 * speed_sq)
        )
        result.append(piece - relaxation * (piece - balance))
    return result


def stream_axis(pieces, component, padder):
    chosen = [index for index, move in enumerate(lattice_moves) if move[component] != 0]
    padded = padder(jnp.stack([pieces[index] for index in chosen]))
    extent = pieces[0].shape[component]
    result = list(pieces)
    for place, index in enumerate(chosen):
        start = 1 - lattice_moves[index][component]
        result[index] = lax.slice_in_dim(padded[place], start, start + extent, axis=component)
    return result


def on_device(populations):
    pieces = [populations[index] for index in range(19)]
    moments = jnp.stack(lattice_moments(pieces))
    file_order = jnp.transpose(moments, (0, 3, 2, 1))
    moments_slab = lax.all_to_all(file_order, "gx", split_axis=1, concat_axis=3, tiled=True)
    read = stream_axis(pieces, 0, lambda part: with_halo(part, (("gx", 1),), 1))
    read = stream_axis(read, 1, lambda part: with_halo(part, (("gy", 2),), 1))
    read = stream_axis(read, 2, lambda part: with_halo(part, (("gz", 3),), 1))
    populations_next = jnp.stack(collide(read))
    return (populations_next, moments_slab)


def solution(mesh):
    return jax.shard_map(
        on_device,
        mesh=mesh,
        in_specs=(P(None, "gx", "gy", "gz"),),
        out_specs=(P(None, "gx", "gy", "gz"), P(None, ("gz", "gx"), "gy", None)),
        check_vma=False,
    )
```

profile of v0, /device:TPU:0, one launch (start us, length us, event | category | flops | bytes accessed | tf_op | source)
XLA Modules:
  0.0 50.1 jit_solution(12742295588593382738)
XLA Ops:
  0.6 0.0 copy-start
  0.6 1.0 %slice.286 = f32[8,8,8,128]{3,2,1,0:T(8,128)S(1)} slice(f32[19,8,8,128]{3,2,1,0:T(8,128)} %param.1), slice={[7:15], [0:8], [0:8], [0:128]} | slice | bytes 524288 | tf_op jit(solution)/shard_map/slice | solution.py:90
  1.7 1.5 %constant_dynamic-update-slice_fusion.4 = (f32[10,8,8,128]{3,2,1,0:T(8,128)}, f32[10,8,8,128]{3,2,1,0:T(8,128)S(1)}, f32[2,8,8,128]{3,2,1,0:T(8,128)S(1)}) fusion(f32[19,8,8,128]{3,2,1,0:T(8,128)} %param.1), kind=kLoop, calls=%fused_computation.8 | loop fusion | bytes 393216
  3.2 7.0 %collective-permute-start.1 = (f32[10,1,8,128]{3,2,1,0:T(8,128)S(1)}, f32[10,1,8,128]{3,2,1,0:T(8,128)S(1)}, u32[]{:S(2)}, u32[]{:S(2)}) collective-permute-start(f32[10,1,8,128]{3,2,1,0:T(8,128)S(1)} %get-tuple-element.45), channel_id=1, source_target_pairs={{2,0},{4,2},{6,4},{8,6},{10,8},{12,10},{14,12},{16,14},{18,16},{20... | collective-permute-start | bytes 122888 | tf_op jit(solution)/shard_map/ppermute | solution.py:40
  10.2 0.0 collective-permute-start
  10.2 1.1 %subtract_divide_fusion.1 = (f32[1,8,8,128]{3,2,1,0:T(8,128)S(1)}, f32[1,8,8,128]{3,2,1,0:T(8,128)S(1)}) fusion(f32[19,8,8,128]{3,2,1,0:T(8,128)} %param.1), kind=kLoop, calls=%fused_computation.241 | loop fusion | flops 229376 | bytes 688128 | tf_op jit(solution)/shard_map/div | solution.py:57
  11.3 0.0 copy-done
  11.4 0.7 %pad_maximum_fusion.2 = f32[4,8,8,128]{3,2,1,0:T(8,128)} fusion(f32[1,8,8,128]{3,2,1,0:T(8,128)S(1)} %add_divide_fusion, f32[1,8,8,128]{3,2,1,0:T(8,128)S(1)} %subtract_divide_fusion, f32[1,8,8,128]{3,2,1,0:T(8,128)S(1)} %get-tuple-element.4, f32[1,8,8,128]{3,2,1,0:T(8,128)S(1)} %get-tuple-element.5), kind=kLoop, calls=%fused_computation.2 | loop fusion | flops 98304 | bytes 262144 | tf_op jit(solution)/shard_map/stack | solution.py:91
  12.1 2.7 %copy.56 = f32[4,8,8,128]{2,1,0,3:T(8,128)S(1)} copy(f32[4,8,8,128]{3,2,1,0:T(8,128)} %pad_maximum_fusion.2) | data formatting | bytes 262144 | tf_op jit(solution)/shard_map/stack | solution.py:91
  14.8 3.0 %collective-permute-done = f32[10,1,8,128]{3,2,1,0:T(8,128)S(1)} collective-permute-done((f32[10,1,8,128]{3,2,1,0:T(8,128)S(1)}, f32[10,1,8,128]{3,2,1,0:T(8,128)S(1)}, u32[]{:S(2)}, u32[]{:S(2)}) %collective-permute-start) | collective-permute-done | bytes 40992 | tf_op jit(solution)/shard_map/ppermute | solution.py:39
  17.8 0.6 %constant_dynamic-update-slice_fusion.3 = f32[10,8,8,128]{3,2,1,0:T(8,128)} fusion(f32[10,8,8,128]{3,2,1,0:T(8,128)} %get-tuple-element.34, f32[10,1,8,128]{3,2,1,0:T(8,128)S(1)} %collective-permute-done, f32[8,8,8,128]{3,2,1,0:T(8,128)S(1)} %slice.286, f32[2,8,8,128]{3,2,1,0:T(8,128)S(1)} %get-tuple-element.36), kind=kLoop, calls=%fused_computation.7 | loop fusion | flops 16384 | bytes 401408
  18.5 0.0 collective-permute-done.1
  18.5 0.6 %constant_dynamic-update-slice_fusion.2 = f32[10,8,8,128]{3,2,1,0:T(8,128)} fusion(f32[10,8,8,128]{3,2,1,0:T(8,128)} %constant_dynamic-update-slice_fusion.3, f32[10,1,8,128]{3,2,1,0:T(8,128)S(1)} %collective-permute-done.1, f32[8,8,8,128]{3,2,1,0:T(8,128)S(1)} %slice.286, f32[2,8,8,128]{3,2,1,0:T(8,128)S(1)} %get-tuple-element.36), kind=kLoop, calls=%fused_computation.6 | loop fusion | flops 16384 | bytes 401408
  19.1 0.6 %constant_dynamic-update-slice_fusion.1 = (f32[10,8,8,128]{3,2,1,0:T(8,128)}, f32[10,8,8,128]{3,2,1,0:T(8,128)S(1)}) fusion(f32[10,8,8,128]{3,2,1,0:T(8,128)} %constant_dynamic-update-slice_fusion.2, f32[10,1,8,128]{3,2,1,0:T(8,128)S(1)} %collective-permute-done, f32[8,8,8,128]{3,2,1,0:T(8,128)S(1)} %slice.286, f32[2,8,8,128]{3,2,1,0:T(8,128)S(1)} %get-tuple-element.36, ...), kind=kLoop, calls=%fused_computation.5 | loop fusion | flops 32768 | bytes 434176
  19.7 0.6 %constant_dynamic-update-slice_fusion = (f32[10,8,8,128]{3,2,1,0:T(8,128)}, f32[10,8,8,128]{3,2,1,0:T(8,128)S(1)}) fusion(f32[10,8,8,128]{3,2,1,0:T(8,128)} %get-tuple-element.39, f32[10,1,8,128]{3,2,1,0:T(8,128)S(1)} %collective-permute-done.1, f32[8,8,8,128]{3,2,1,0:T(8,128)S(1)} %slice.286, f32[2,8,8,128]{3,2,1,0:T(8,128)S(1)} %get-tuple-element.36, ...), kind=kLoop, calls=%fused_computation.4 | loop fusion | flops 32768 | bytes 434176
  20.3 0.7 %slice_dynamic-update-slice_fusion = f32[10,8,8,128]{3,2,1,0:T(8,128)} fusion(f32[10,8,8,128]{3,2,1,0:T(8,128)} %get-tuple-element.37, f32[19,8,8,128]{3,2,1,0:T(8,128)S(1)} %copy-done), kind=kLoop, calls=%fused_computation.3 | loop fusion | bytes 262144 | tf_op jit(solution)/shard_map/stack | solution.py:80
  21.0 1.1 %fusion.152 = (f32[10,8,1,128]{3,2,1,0:T(1,128)S(1)}, f32[10,8,1,128]{3,2,1,0:T(1,128)S(1)}) fusion(f32[10,8,8,128]{3,2,1,0:T(8,128)} %slice_dynamic-update-slice_fusion), kind=kLoop, calls=%fused_computation.254 | loop fusion | bytes 163840 | tf_op jit(solution)/shard_map/slice | solution.py:37
  22.1 0.0 collective-permute-start.3
  22.1 0.0 collective-permute-start.2
  22.2 0.0 collective-permute-done.3
  22.2 0.0 collective-permute-done.2
  22.2 1.1 %pad_maximum_fusion = f32[10,8,10,128]{3,2,1,0:T(8,128)S(1)} fusion(f32[10,8,1,128]{3,2,1,0:T(1,128)S(1)} %bitcast.192, f32[10,8,8,128]{3,2,1,0:T(8,128)} %slice_dynamic-update-slice_fusion, f32[10,8,1,128]{3,2,1,0:T(1,128)S(1)} %bitcast.193), kind=kLoop, calls=%fused_computation | loop fusion | flops 204800 | bytes 819200 | tf_op jit(solution)/shard_map/concatenate | solution.py:41
  23.3 0.7 %slice_bitcast_fusion.19 = (f32[8,10,128]{2,1,0:T(8,128)}, f32[8,10,128]{2,1,0:T(8,128)S(1)}, f32[8,10,128]{2,1,0:T(8,128)}, f32[8,10,128]{2,1,0:T(8,128)}, f32[...) fusion(f32[10,8,10,128]{3,2,1,0:T(8,128)S(1)} %pad_maximum_fusion), kind=kLoop, calls=%fused_computation.56 | loop fusion | bytes 819200 | tf_op jit(solution)/shard_map/squeeze | solution.py:85
  24.1 0.9 %fusion.151 = (f32[10,8,8,1]{3,2,1,0:T(8,128)}, f32[10,8,8,1]{3,2,1,0:T(8,128)}) fusion(f32[10,8,8,128]{3,2,1,0:T(8,128)S(1)} %constant_dynamic-update-slice_fusion.5), kind=kLoop, calls=%fused_computation.253 | loop fusion | bytes 10240 | tf_op jit(solution)/shard_map/slice | solution.py:37
  25.0 0.0 collective-permute-start.4
  25.0 0.5 %collective-permute-start.5 = (f32[10,8,8,1]{3,2,1,0:T(8,128)}, f32[10,8,8,1]{3,2,1,0:T(8,128)}, u32[]{:S(2)}, u32[]{:S(2)}) collective-permute-start(f32[10,8,8,1]{3,2,1,0:T(8,128)} %get-tuple-element.42), channel_id=1, source_target_pairs={{1,0},{0,1},{3,2},{2,3},{5,4},{4,5},{7,6},{6,7},{9,8},{8,9},{11,10... | collective-permute-start | bytes 7688 | tf_op jit(solution)/shard_map/ppermute | solution.py:40
  25.5 1.5 %bitcast_bitcast_fusion = f32[128,4,8,8]{3,2,1,0:T(8,128)} fusion(f32[4,8,8,128]{2,1,0,3:T(8,128)S(1)} %copy.56), kind=kLoop, calls=%fused_computation.255 | loop fusion | bytes 262144
  27.0 3.3 %reshape.22 = f32[16,1,2048]{2,1,0:T(1,128)} reshape(f32[128,4,8,8]{3,2,1,0:T(8,128)} %bitcast_bitcast_fusion) | data formatting | bytes 262144
  30.4 0.0 copy-start.5
  30.4 4.1 %all-to-all-start = ((f32[16,1,2048]{2,1,0:T(1,128)}), f32[16,1,2048]{2,1,0:T(1,128)S(1)}, u32[]{:S(2)}, u32[]{:S(2)}) async-start(f32[16,1,2048]{2,1,0:T(1,128)} %reshape.22), calls=%async_computation | async-start | bytes 262144 | tf_op jit(solution)/shard_map/all_to_all | solution.py:93
  34.5 0.0 collective-permute-done.4
  34.5 0.0 collective-permute-done.5
  34.6 1.4 %pad_maximum_fusion.1 = f32[10,8,8,130]{3,2,1,0:T(8,128)S(1)} fusion(f32[10,8,8,1]{3,2,1,0:T(8,128)} %collective-permute-done.5, f32[10,8,8,128]{3,2,1,0:T(8,128)S(1)} %constant_dynamic-update-slice_fusion.5, f32[10,8,8,1]{3,2,1,0:T(8,128)} %collective-permute-done.4), kind=kLoop, calls=%fused_computation.1 | loop fusion | flops 166400 | bytes 665600 | tf_op jit(solution)/shard_map/concatenate | solution.py:41
  36.0 0.0 copy-done.1
  36.0 0.0 copy-done.2
  36.1 0.2 constant_dynamic-update-slice_fusion.32
  36.4 0.1 constant_dynamic-update-slice_fusion.26
  36.6 0.1 constant_dynamic-update-slice_fusion.20
  36.7 0.1 constant_dynamic-update-slice_fusion.19
  36.9 0.1 constant_dynamic-update-slice_fusion.16
  37.0 0.1 constant_dynamic-update-slice_fusion.15
  37.1 0.0 copy-start.6
  37.1 5.3 %all-to-all-done = f32[16,1,2048]{2,1,0:T(1,128)S(1)} async-done(((f32[16,1,2048]{2,1,0:T(1,128)}), f32[16,1,2048]{2,1,0:T(1,128)S(1)}, u32[]{:S(2)}, u32[]{:S(2)}) %all-to-all-start) | async-done | bytes 131104 | tf_op jit(solution)/shard_map/all_to_all | solution.py:93
  42.3 0.5 %broadcast.211 = f32[]{:T(128)} broadcast(f32[]{:T(128)} %constant.332), dimensions={} | broadcast | bytes 8 | tf_op jit(solution)/shard_map/all_to_all | solution.py:93
  42.9 0.9 %reduce = f32[16,2048]{1,0:T(8,128)S(1)} reduce(f32[16,1,2048]{2,1,0:T(1,128)S(1)} %all-to-all-done, f32[]{:T(128)} %broadcast.211), dimensions={1}, to_apply=%all_to_all.13.reduce_sub_computation | reduce | bytes 262148 | tf_op jit(solution)/shard_map/all_to_all | solution.py:93
  43.8 1.1 %reshape.23 = f32[128,4,8,8]{3,2,1,0:T(8,128)S(1)} reshape(f32[16,2048]{1,0:T(8,128)S(1)} %reduce) | data formatting | bytes 262144
  45.0 1.9 %copy.58 = f32[4,8,8,16,8]{4,3,2,1,0:T(8,128)} copy(f32[4,8,8,16,8]{2,4,0,1,3:T(8,128)S(1)} %bitcast.191) | data formatting | bytes 262144 | tf_op jit(solution)/shard_map/all_to_all | solution.py:93
  46.8 3.2 %all_to_all.16 = f32[4,8,8,128]{3,2,1,0:T(8,128)} reshape(f32[4,8,8,16,8]{4,3,2,1,0:T(8,128)} %copy.58) | data formatting | bytes 262144 | tf_op jit(solution)/shard_map/all_to_all | solution.py:93
  (31 shorter events, 0.5 us)
Async XLA Ops:
  0.6 10.7 %copy-start = (f32[19,8,8,128]{3,2,1,0:T(8,128)S(1)}, f32[19,8,8,128]{3,2,1,0:T(8,128)}, u32[]{:S(2)}) copy-start(f32[19,8,8,128]{3,2,1,0:T(8,128)} %param.1) | copy-start | bytes 1867780
  3.2 15.2 %collective-permute-start.1 = (f32[10,1,8,128]{3,2,1,0:T(8,128)S(1)}, f32[10,1,8,128]{3,2,1,0:T(8,128)S(1)}, u32[]{:S(2)}, u32[]{:S(2)}) collective-permute-start(f32[10,1,8,128]{3,2,1,0:T(8,128)S(1)} %get-tuple-element.45), channel_id=1, source_target_pairs={{2,0},{4,2},{6,4},{8,6},{10,8},{12,10},{14,12},{16,14},{18,16},{20... | collective-permute-start | bytes 122888 | tf_op jit(solution)/shard_map/ppermute | solution.py:40
  10.2 7.6 %collective-permute-start = (f32[10,1,8,128]{3,2,1,0:T(8,128)S(1)}, f32[10,1,8,128]{3,2,1,0:T(8,128)S(1)}, u32[]{:S(2)}, u32[]{:S(2)}) collective-permute-start(f32[10,1,8,128]{3,2,1,0:T(8,128)S(1)} %get-tuple-element.46), channel_id=1, source_target_pairs={{0,2},{2,4},{4,6},{6,8},{8,10},{10,12},{12,14},{14,16},{16,18},{18... | collective-permute-start | bytes 122888 | tf_op jit(solution)/shard_map/ppermute | solution.py:39
  22.1 0.1 collective-permute-start.3
  22.1 0.1 collective-permute-start.2
  25.0 9.5 %collective-permute-start.4 = (f32[10,8,8,1]{3,2,1,0:T(8,128)}, f32[10,8,8,1]{3,2,1,0:T(8,128)}, u32[]{:S(2)}, u32[]{:S(2)}) collective-permute-start(f32[10,8,8,1]{3,2,1,0:T(8,128)} %get-tuple-element.41), channel_id=1, source_target_pairs={{0,1},{1,0},{2,3},{3,2},{4,5},{5,4},{6,7},{7,6},{8,9},{9,8},{10,11... | collective-permute-start | bytes 7688 | tf_op jit(solution)/shard_map/ppermute | solution.py:39
  25.0 9.5 %collective-permute-start.5 = (f32[10,8,8,1]{3,2,1,0:T(8,128)}, f32[10,8,8,1]{3,2,1,0:T(8,128)}, u32[]{:S(2)}, u32[]{:S(2)}) collective-permute-start(f32[10,8,8,1]{3,2,1,0:T(8,128)} %get-tuple-element.42), channel_id=1, source_target_pairs={{1,0},{0,1},{3,2},{2,3},{5,4},{4,5},{7,6},{6,7},{9,8},{8,9},{11,10... | collective-permute-start | bytes 7688 | tf_op jit(solution)/shard_map/ppermute | solution.py:40
  30.4 5.6 %copy-start.1 = (f32[8,10,128]{2,1,0:T(8,128)S(1)}, f32[8,10,128]{2,1,0:T(8,128)}, u32[]{:S(2)}) copy-start(f32[8,10,128]{2,1,0:T(8,128)} %get-tuple-element.26) | copy-start | bytes 122884
  30.4 5.6 %copy-start.2 = (f32[8,10,128]{2,1,0:T(8,128)S(1)}, f32[8,10,128]{2,1,0:T(8,128)}, u32[]{:S(2)}) copy-start(f32[8,10,128]{2,1,0:T(8,128)} %get-tuple-element.27) | copy-start | bytes 122884
  30.4 5.6 %copy-start.3 = (f32[8,10,128]{2,1,0:T(8,128)S(1)}, f32[8,10,128]{2,1,0:T(8,128)}, u32[]{:S(2)}) copy-start(f32[8,10,128]{2,1,0:T(8,128)} %get-tuple-element.28) | copy-start | bytes 122884
  30.4 5.7 %copy-start.4 = (f32[8,10,128]{2,1,0:T(8,128)S(1)}, f32[8,10,128]{2,1,0:T(8,128)}, u32[]{:S(2)}) copy-start(f32[8,10,128]{2,1,0:T(8,128)} %get-tuple-element.33) | copy-start | bytes 122884
  30.4 5.7 %copy-start.5 = (f32[8,10,128]{2,1,0:T(8,128)S(1)}, f32[8,10,128]{2,1,0:T(8,128)}, u32[]{:S(2)}) copy-start(f32[8,10,128]{2,1,0:T(8,128)} %get-tuple-element.24) | copy-start | bytes 122884
  30.4 11.9 %all-to-all-start = ((f32[16,1,2048]{2,1,0:T(1,128)}), f32[16,1,2048]{2,1,0:T(1,128)S(1)}, u32[]{:S(2)}, u32[]{:S(2)}) async-start(f32[16,1,2048]{2,1,0:T(1,128)} %reshape.22), calls=%async_computation | async-start | bytes 262144 | tf_op jit(solution)/shard_map/all_to_all | solution.py:93
  37.1 5.8 %copy-start.6 = (f32[19,8,8,128]{3,2,1,0:T(8,128)}, f32[19,8,8,128]{3,2,1,0:T(8,128)S(1)}, u32[]{:S(2)}) copy-start(f32[19,8,8,128]{3,2,1,0:T(8,128)S(1)} %constant_dynamic-update-slice_fusion.14) | copy-start | bytes 1867780
where the time goes:
time: 50.6 us; the launch traced here: 50.1 us
  local copies, waits for them, and re-layouts  20.5 us (41%)
  starting transfers between devices  11.7 us (23%)
  other arithmetic  8.69 us (17%)
  waiting for transfers between devices  8.31 us (16%)
  between operations  0.93 us (2%)
    unnamed x21, local copies, waits for them, and re-layouts  7.58 us
    ppermute x3, starting transfers between devices, with_halo(): after = lax.ppermute(leading, axis, down)  7.52 us
    all_to_all x3, local copies, waits for them, and re-layouts, on_device(): lax.all_to_all(file_order, 'gx', split_axis=1, concat_axis=3, tiled=True)  5.64 us
    all_to_all x1, waiting for transfers between devices, on_device(): lax.all_to_all(file_order, 'gx', split_axis=1, concat_axis=3, tiled=True)  5.26 us
    all_to_all x1, starting transfers between devices, on_device(): lax.all_to_all(file_order, 'gx', split_axis=1, concat_axis=3, tiled=True)  4.12 us
    unnamed x24, other arithmetic  3.4 us
    ppermute x3, waiting for transfers between devices, with_halo(): before = lax.ppermute(last, axis, up)  3.04 us
    another operation x1, local copies, waits for them, and re-layouts, on_device(): moments = jnp.stack(lattice_moments(pieces))  2.72 us
  transfers between devices with their start and end apart: 7, of which 2 were waited for; matrix products, arithmetic and copies ran while one was open for 25% of the time, Pallas kernels for 0%

commit v1 on v0

--- a/solution.py
+++ b/solution.py
@@ -90,7 +90,9 @@
     pieces = [populations[index] for index in range(19)]
     moments = jnp.stack(lattice_moments(pieces))
     file_order = jnp.transpose(moments, (0, 3, 2, 1))
-    moments_slab = lax.all_to_all(file_order, "gx", split_axis=1, concat_axis=3, tiled=True)
+    parts = jnp.split(file_order, lax.axis_size("gx"), axis=1)
+    received = lax.all_to_all(jnp.stack(parts), "gx", 0, 0)
+    moments_slab = jnp.concatenate(received, axis=3)
     read = stream_axis(pieces, 0, lambda part: with_halo(part, (("gx", 1),), 1))
     read = stream_axis(read, 1, lambda part: with_halo(part, (("gy", 2),), 1))
     read = stream_axis(read, 2, lambda part: with_halo(part, (("gz", 3),), 1))

time: 50.6 us -> 40.1 us (0.79)
  local copies, waits for them, and re-layouts: 20.5 us -> 14.6 us
  other arithmetic: 8.69 us -> 4.61 us
  waiting for transfers between devices: 8.31 us -> 5.28 us
  starting transfers between devices: 11.7 us -> 14 us
    reshape x0 -> x3, local copies, waits for them, and re-layouts: none -> 6.01 us  [on_device(): moments_slab = jnp.concatenate(received, axis=3)]
    all_to_all x3 -> x1, local copies, waits for them, and re-layouts: 5.64 us -> 0.51 us  [on_device(): received = lax.all_to_all(jnp.stack(parts), 'gx', 0, 0)]
    ppermute x3, waiting for transfers between devices: 3.04 us -> 0.01 us  [with_halo(): before = lax.ppermute(last, axis, up)]
    ppermute x3, starting transfers between devices: 0.01 us -> 3.03 us  [with_halo(): before = lax.ppermute(last, axis, up)]
    ppermute x3, starting transfers between devices: 7.52 us -> 4.57 us  [with_halo(): after = lax.ppermute(leading, axis, down)]
    another operation x1, local copies, waits for them, and re-layouts: 2.72 us -> 0.09 us  [on_device(): received = lax.all_to_all(jnp.stack(parts), 'gx', 0, 0)]
    unnamed x24, other arithmetic: 3.4 us -> 0.96 us
    unnamed x21 -> x35, local copies, waits for them, and re-layouts: 7.58 us -> 5.24 us
  transfers between devices with their start and end apart: 7 -> 7, of which waited for: 2 -> 1; matrix products, arithmetic and copies ran while one was open for 25% -> 17% of each run, Pallas kernels for 0% -> 0%
where the time goes in v1:
time: 40.1 us; the launch traced here: 39.6 us
  local copies, waits for them, and re-layouts  14.6 us (36%)
  starting transfers between devices  14 us (35%)
  waiting for transfers between devices  5.28 us (13%)
  other arithmetic  4.61 us (11%)
  between operations  1.12 us (3%)
    all_to_all x1, starting transfers between devices, on_device(): received = lax.all_to_all(jnp.stack(parts), 'gx', 0, 0)  6.42 us
    reshape x3, local copies, waits for them, and re-layouts, on_device(): moments_slab = jnp.concatenate(received, axis=3)  6.01 us
    all_to_all x1, waiting for transfers between devices, on_device(): received = lax.all_to_all(jnp.stack(parts), 'gx', 0, 0)  5.27 us
    unnamed x35, local copies, waits for them, and re-layouts  5.24 us
    ppermute x3, starting transfers between devices, with_halo(): after = lax.ppermute(leading, axis, down)  4.57 us
    ppermute x3, starting transfers between devices, with_halo(): before = lax.ppermute(last, axis, up)  3.03 us
    concatenate x2, other arithmetic, with_halo(): x = jnp.concatenate([before, x, after], axis=dim)  1.52 us
    div x1, other arithmetic, lattice_moments(): velocity_x = signed_total(pieces, 0) / density  1.09 us
  transfers between devices with their start and end apart: 7, of which 1 were waited for; matrix products, arithmetic and copies ran while one was open for 17% of the time, Pallas kernels for 0%

profile of v1, /device:TPU:0, one launch (start us, length us, event | category | flops | bytes accessed | tf_op | source)
XLA Modules:
  0.0 39.6 jit_solution(14383960465926394549)
XLA Ops:
  0.6 0.0 copy-start
  0.6 1.0 %constant_dynamic-update-slice_fusion.4 = (f32[10,8,8,128]{3,2,1,0:T(8,128)S(1)}, f32[10,8,8,128]{3,2,1,0:T(8,128)S(1)}, f32[2,8,8,128]{3,2,1,0:T(8,128)S(1)}) fusion(f32[19,8,8,128]{3,2,1,0:T(8,128)} %param.1), kind=kLoop, calls=%fused_computation.40 | loop fusion | bytes 393216
  1.6 1.0 %slice.286 = f32[8,8,8,128]{3,2,1,0:T(8,128)S(1)} slice(f32[19,8,8,128]{3,2,1,0:T(8,128)} %param.1), slice={[7:15], [0:8], [0:8], [0:128]} | slice | bytes 524288 | tf_op jit(solution)/shard_map/slice | solution.py:90
  2.6 3.0 %collective-permute-start = (f32[10,1,8,128]{3,2,1,0:T(8,128)S(1)}, f32[10,1,8,128]{3,2,1,0:T(8,128)S(1)}, u32[]{:S(2)}, u32[]{:S(2)}) collective-permute-start(f32[10,1,8,128]{3,2,1,0:T(8,128)S(1)} %get-tuple-element.44), channel_id=1, source_target_pairs={{0,2},{2,4},{4,6},{6,8},{8,10},{10,12},{12,14},{14,16},{16,18},{18... | collective-permute-start | bytes 122888 | tf_op jit(solution)/shard_map/ppermute | solution.py:39
  5.6 4.1 %collective-permute-start.1 = (f32[10,1,8,128]{3,2,1,0:T(8,128)S(1)}, f32[10,1,8,128]{3,2,1,0:T(8,128)S(1)}, u32[]{:S(2)}, u32[]{:S(2)}) collective-permute-start(f32[10,1,8,128]{3,2,1,0:T(8,128)S(1)} %get-tuple-element.43), channel_id=1, source_target_pairs={{2,0},{4,2},{6,4},{8,6},{10,8},{12,10},{14,12},{16,14},{18,16},{20... | collective-permute-start | bytes 122888 | tf_op jit(solution)/shard_map/ppermute | solution.py:40
  9.7 1.1 %subtract_divide_fusion.1 = (f32[1,8,8,128]{3,2,1,0:T(8,128)S(1)}, f32[1,8,8,128]{3,2,1,0:T(8,128)S(1)}) fusion(f32[19,8,8,128]{3,2,1,0:T(8,128)} %param.1), kind=kLoop, calls=%fused_computation.273 | loop fusion | flops 229376 | bytes 688128 | tf_op jit(solution)/shard_map/div | solution.py:57
  10.9 0.1 fusion.14
  11.0 0.1 fusion.13
  11.1 0.1 fusion.12
  11.2 0.1 fusion.11
  11.3 0.1 fusion.10
  11.4 0.1 fusion.9
  11.5 0.1 fusion.8
  11.6 0.1 fusion.7
  11.7 0.1 fusion.6
  11.8 0.1 fusion.5
  11.9 0.1 fusion.4
  12.0 0.1 fusion.3
  12.1 0.1 fusion.2
  12.2 0.1 fusion.1
  12.3 0.0 collective-permute-done
  12.4 0.1 fusion.168
  12.5 0.0 collective-permute-start.2
  12.5 0.0 collective-permute-start.3
  12.6 0.0 collective-permute-done.2
  12.6 0.0 collective-permute-done.3
  12.6 0.1 pad_maximum_fusion
  12.7 0.7 %slice_bitcast_fusion.35 = (f32[8,10,128]{2,1,0:T(8,128)}, f32[8,10,128]{2,1,0:T(8,128)S(1)}, f32[8,10,128]{2,1,0:T(8,128)}, f32[8,10,128]{2,1,0:T(8,128)}, f32[...) fusion(f32[10,8,10,128]{3,2,1,0:T(8,128)S(1)} %pad_maximum_fusion), kind=kLoop, calls=%fused_computation.88 | loop fusion | bytes 819200 | tf_op jit(solution)/shard_map/squeeze | solution.py:85
  13.5 0.9 %fusion.167 = (f32[10,8,8,1]{3,2,1,0:T(8,128)}, f32[10,8,8,1]{3,2,1,0:T(8,128)}) fusion(f32[10,8,8,128]{3,2,1,0:T(8,128)S(1)} %constant_dynamic-update-slice_fusion.5), kind=kLoop, calls=%fused_computation.285 | loop fusion | bytes 10240 | tf_op jit(solution)/shard_map/slice | solution.py:37
  14.4 0.5 %collective-permute-start.5 = (f32[10,8,8,1]{3,2,1,0:T(8,128)}, f32[10,8,8,1]{3,2,1,0:T(8,128)}, u32[]{:S(2)}, u32[]{:S(2)}) collective-permute-start(f32[10,8,8,1]{3,2,1,0:T(8,128)} %get-tuple-element.40), channel_id=1, source_target_pairs={{1,0},{0,1},{3,2},{2,3},{5,4},{4,5},{7,6},{6,7},{9,8},{8,9},{11,10... | collective-permute-start | bytes 7688 | tf_op jit(solution)/shard_map/ppermute | solution.py:40
  14.9 0.1 fusion
  15.0 1.7 %reshape.30 = f32[16,1,2048]{2,1,0:T(1,128)} reshape(f32[16,4,8,8,8]{4,3,2,1,0:T(8,128)S(1)} %bitcast.249) | data formatting | bytes 262144
  16.8 6.4 %all-to-all-start = ((f32[16,1,2048]{2,1,0:T(1,128)}), f32[16,1,2048]{2,1,0:T(1,128)S(1)}, u32[]{:S(2)}, u32[]{:S(2)}) async-start(f32[16,1,2048]{2,1,0:T(1,128)} %reshape.30), calls=%async_computation | async-start | bytes 262144 | tf_op jit(solution)/shard_map/all_to_all | solution.py:94
  23.2 1.4 %pad_maximum_fusion.1 = f32[10,8,8,130]{3,2,1,0:T(8,128)S(1)} fusion(f32[10,8,8,1]{3,2,1,0:T(8,128)} %collective-permute-done.5, f32[10,8,8,128]{3,2,1,0:T(8,128)S(1)} %constant_dynamic-update-slice_fusion.5, f32[10,8,8,1]{3,2,1,0:T(8,128)} %collective-permute-done.4), kind=kLoop, calls=%fused_computation.1 | loop fusion | flops 166400 | bytes 665600 | tf_op jit(solution)/shard_map/concatenate | solution.py:41
  24.7 0.2 constant_dynamic-update-slice_fusion.32
  25.1 0.1 constant_dynamic-update-slice_fusion.26
  25.3 0.1 constant_dynamic-update-slice_fusion.20
  25.4 0.1 constant_dynamic-update-slice_fusion.19
  25.5 0.1 constant_dynamic-update-slice_fusion.16
  25.6 0.1 constant_dynamic-update-slice_fusion.15
  25.7 0.0 copy-start.6
  25.7 5.3 %all-to-all-done = f32[16,1,2048]{2,1,0:T(1,128)S(1)} async-done(((f32[16,1,2048]{2,1,0:T(1,128)}), f32[16,1,2048]{2,1,0:T(1,128)S(1)}, u32[]{:S(2)}, u32[]{:S(2)}) %all-to-all-start) | async-done | bytes 131104 | tf_op jit(solution)/shard_map/all_to_all | solution.py:94
  31.0 0.5 %broadcast.211 = f32[]{:T(128)} broadcast(f32[]{:T(128)} %constant.379), dimensions={} | broadcast | bytes 8 | tf_op jit(solution)/shard_map/all_to_all | solution.py:94
  31.5 0.9 %reduce = f32[16,2048]{1,0:T(8,128)S(1)} reduce(f32[16,1,2048]{2,1,0:T(1,128)S(1)} %all-to-all-done, f32[]{:T(128)} %broadcast.211), dimensions={1}, to_apply=%all_to_all.3.reduce_sub_computation | reduce | bytes 262148 | tf_op jit(solution)/shard_map/all_to_all | solution.py:94
  32.5 1.1 %reshape.31 = f32[16,4,8,8,8]{4,3,2,1,0:T(8,128)S(1)} reshape(f32[16,2048]{1,0:T(8,128)S(1)} %reduce) | data formatting | bytes 262144
  33.6 1.5 %bitcast_bitcast_fusion = f32[4,8,8,16,8]{1,2,4,0,3:T(8,128)} fusion(f32[16,4,8,8,8]{4,3,2,1,0:T(8,128)S(1)} %reshape.31), kind=kLoop, calls=%fused_computation.287 | loop fusion | bytes 262144 | tf_op jit(solution)/shard_map/reshape | solution.py:95
  35.1 2.9 %copy.4 = f32[4,8,8,16,8]{4,3,2,1,0:T(8,128)S(1)} copy(f32[4,8,8,16,8]{1,2,4,0,3:T(8,128)} %bitcast_bitcast_fusion) | data formatting | bytes 262144 | tf_op jit(solution)/shard_map/reshape | solution.py:95
  38.0 1.6 %reshape.29 = f32[4,8,8,128]{3,2,1,0:T(8,128)} reshape(f32[4,8,8,16,8]{4,3,2,1,0:T(8,128)S(1)} %copy.4) | data formatting | bytes 262144 | tf_op jit(solution)/shard_map/reshape | solution.py:95
  (46 shorter events, 0.6 us)
Async XLA Ops:
  0.6 10.2 %copy-start = (f32[19,8,8,128]{3,2,1,0:T(8,128)S(1)}, f32[19,8,8,128]{3,2,1,0:T(8,128)}, u32[]{:S(2)}) copy-start(f32[19,8,8,128]{3,2,1,0:T(8,128)} %param.1) | copy-start | bytes 1867780
  2.6 9.7 %collective-permute-start = (f32[10,1,8,128]{3,2,1,0:T(8,128)S(1)}, f32[10,1,8,128]{3,2,1,0:T(8,128)S(1)}, u32[]{:S(2)}, u32[]{:S(2)}) collective-permute-start(f32[10,1,8,128]{3,2,1,0:T(8,128)S(1)} %get-tuple-element.44), channel_id=1, source_target_pairs={{0,2},{2,4},{4,6},{6,8},{8,10},{10,12},{12,14},{14,16},{16,18},{18... | collective-permute-start | bytes 122888 | tf_op jit(solution)/shard_map/ppermute | solution.py:39
  5.6 6.7 %collective-permute-start.1 = (f32[10,1,8,128]{3,2,1,0:T(8,128)S(1)}, f32[10,1,8,128]{3,2,1,0:T(8,128)S(1)}, u32[]{:S(2)}, u32[]{:S(2)}) collective-permute-start(f32[10,1,8,128]{3,2,1,0:T(8,128)S(1)} %get-tuple-element.43), channel_id=1, source_target_pairs={{2,0},{4,2},{6,4},{8,6},{10,8},{12,10},{14,12},{16,14},{18,16},{20... | collective-permute-start | bytes 122888 | tf_op jit(solution)/shard_map/ppermute | solution.py:40
  12.5 0.1 collective-permute-start.2
  12.5 0.1 collective-permute-start.3
  14.4 8.8 %collective-permute-start.4 = (f32[10,8,8,1]{3,2,1,0:T(8,128)}, f32[10,8,8,1]{3,2,1,0:T(8,128)}, u32[]{:S(2)}, u32[]{:S(2)}) collective-permute-start(f32[10,8,8,1]{3,2,1,0:T(8,128)} %get-tuple-element.39), channel_id=1, source_target_pairs={{0,1},{1,0},{2,3},{3,2},{4,5},{5,4},{6,7},{7,6},{8,9},{9,8},{10,11... | collective-permute-start | bytes 7688 | tf_op jit(solution)/shard_map/ppermute | solution.py:39
  14.4 8.8 %collective-permute-start.5 = (f32[10,8,8,1]{3,2,1,0:T(8,128)}, f32[10,8,8,1]{3,2,1,0:T(8,128)}, u32[]{:S(2)}, u32[]{:S(2)}) collective-permute-start(f32[10,8,8,1]{3,2,1,0:T(8,128)} %get-tuple-element.40), channel_id=1, source_target_pairs={{1,0},{0,1},{3,2},{2,3},{5,4},{4,5},{7,6},{6,7},{9,8},{8,9},{11,10... | collective-permute-start | bytes 7688 | tf_op jit(solution)/shard_map/ppermute | solution.py:40
  16.8 7.9 %copy-start.1 = (f32[8,10,128]{2,1,0:T(8,128)S(1)}, f32[8,10,128]{2,1,0:T(8,128)}, u32[]{:S(2)}) copy-start(f32[8,10,128]{2,1,0:T(8,128)} %get-tuple-element.24) | copy-start | bytes 122884
  16.8 7.9 %copy-start.2 = (f32[8,10,128]{2,1,0:T(8,128)S(1)}, f32[8,10,128]{2,1,0:T(8,128)}, u32[]{:S(2)}) copy-start(f32[8,10,128]{2,1,0:T(8,128)} %get-tuple-element.25) | copy-start | bytes 122884
  16.8 7.9 %copy-start.3 = (f32[8,10,128]{2,1,0:T(8,128)S(1)}, f32[8,10,128]{2,1,0:T(8,128)}, u32[]{:S(2)}) copy-start(f32[8,10,128]{2,1,0:T(8,128)} %get-tuple-element.26) | copy-start | bytes 122884
  16.8 8.0 %copy-start.4 = (f32[8,10,128]{2,1,0:T(8,128)S(1)}, f32[8,10,128]{2,1,0:T(8,128)}, u32[]{:S(2)}) copy-start(f32[8,10,128]{2,1,0:T(8,128)} %get-tuple-element.31) | copy-start | bytes 122884
  16.8 8.0 %copy-start.5 = (f32[8,10,128]{2,1,0:T(8,128)S(1)}, f32[8,10,128]{2,1,0:T(8,128)}, u32[]{:S(2)}) copy-start(f32[8,10,128]{2,1,0:T(8,128)} %get-tuple-element.22) | copy-start | bytes 122884
  16.8 14.2 %all-to-all-start = ((f32[16,1,2048]{2,1,0:T(1,128)}), f32[16,1,2048]{2,1,0:T(1,128)S(1)}, u32[]{:S(2)}, u32[]{:S(2)}) async-start(f32[16,1,2048]{2,1,0:T(1,128)} %reshape.30), calls=%async_computation | async-start | bytes 262144 | tf_op jit(solution)/shard_map/all_to_all | solution.py:94
  25.7 9.4 %copy-start.6 = (f32[19,8,8,128]{3,2,1,0:T(8,128)}, f32[19,8,8,128]{3,2,1,0:T(8,128)S(1)}, u32[]{:S(2)}) copy-start(f32[19,8,8,128]{3,2,1,0:T(8,128)S(1)} %constant_dynamic-update-slice_fusion.14) | copy-start | bytes 1867780
